TPU v7x, 16 devices: a 4x2x1 block of a 4x4x8 slice. The times are simulated.
16 devices in a mesh: sweep: 2 (over y, z), ent: 8 (over x, core).
Axes of the slice: x: 4, y: 2, z: 1, core: 2. Of those that a mesh axis runs over, the one named last changes fastest.
The devices are a block of a 4x4x8 slice.
Arguments:
- ent_table: float32 [65536, 200], P(('sweep', 'ent')), parts along dimension 0
- ent_accum: float32 [65536], P(('sweep', 'ent')), parts along dimension 0
- rel_table: float32 [22, 200], P('sweep'), parts along dimension 0
- rel_accum: float32 [22], P('sweep'), parts along dimension 0
- head_idx: int32 [16, 8, 2048], P(('sweep', 'ent')), parts along dimension 0
- tail_idx: int32 [16, 8, 2048], P(('sweep', 'ent')), parts along dimension 0
- rel_idx: int32 [16, 8, 2048], P(('sweep', 'ent')), parts along dimension 0
- edge_mask: int32 [16, 8, 2048], P(('sweep', 'ent')), parts along dimension 0
- neg_idx: int32 [16, 8, 2048], P(('sweep', 'ent')), parts along dimension 0
Outputs:
- output 1: float32 [65536, 200], P(('sweep', 'ent')), parts along dimension 0
- output 2: float32 [65536], P(('sweep', 'ent')), parts along dimension 0
- output 3: float32 [22, 200], P('sweep'), parts along dimension 0
- output 4: float32 [22], P('sweep'), parts along dimension 0
- output 5: float32 [16, 8], P(('sweep', 'ent')), parts along dimension 0
There are 2 independent parts. A program takes and returns all parts, laid end to end along the dimension named above; each array names one.
All inputs are finite; a program needn't handle non-finite values.
Results may differ from a plain program's by a relative error of at most 0.001.
Values are sent between devices in bfloat16 or wider.
A program may use at most 768 MiB of HBM per device.

v0:
```python
import jax
import jax.numpy as jnp
from jax import lax
from jax.sharding import PartitionSpec as P

LR_ENT = 0.03
LR_REL = 0.05
ADA_EPS = 1e-10


def complex_mul(left_op, right_op):
    half_dim = left_op.shape[-1] // 2
    left_re, left_im = left_op[..., :half_dim], left_op[..., half_dim:]
    right_re, right_im = right_op[..., :half_dim], right_op[..., half_dim:]
    return jnp.concatenate([left_re * right_re - left_im * right_im, left_re * right_im + left_im * right_re], axis=-1)


def conj_mul(grad_in, other_op):
    half_dim = grad_in.shape[-1] // 2
    grad_re, grad_im = grad_in[..., :half_dim], grad_in[..., half_dim:]
    other_re, other_im = other_op[..., :half_dim], other_op[..., half_dim:]
    return jnp.concatenate([grad_re * other_re + grad_im * other_im, grad_im * other_re - grad_re * other_im], axis=-1)


def adagrad(param_rows, accum_rows, grad_rows, step_rate):
    new_accum = accum_rows + jnp.mean(grad_rows * grad_rows, axis=1)
    new_param = param_rows - step_rate * grad_rows / jnp.sqrt(new_accum + ADA_EPS)[:, None]
    return new_param, new_accum


def bucket_grads(head_rows, rel_rows, tail_rows, neg_rows, edge_w):
    query_bf = complex_mul(head_rows, rel_rows).astype(jnp.bfloat16)
    pos_score = jnp.einsum("bd,bd->b", query_bf, tail_rows, preferred_element_type=jnp.float32)
    neg_score = lax.dot_general(query_bf, neg_rows, (((1,), (1,)), ((), ())), preferred_element_type=jnp.float32)
    logits = jnp.concatenate([pos_score[:, None], neg_score], axis=1)
    log_norm = jax.nn.logsumexp(logits, axis=1)
    weight = edge_w.astype(jnp.float32)
    round_loss = jnp.sum(weight * (log_norm - pos_score)) / edge_w.shape[0]
    soft_w = jnp.exp(logits - log_norm[:, None])
    d_pos = weight * (soft_w[:, 0] - 1.0)
    d_neg = (weight[:, None] * soft_w[:, 1:]).astype(jnp.bfloat16)
    d_query = d_pos[:, None] * tail_rows + jnp.dot(d_neg, neg_rows, preferred_element_type=jnp.float32)
    d_negrows = lax.dot_general(d_neg, query_bf, (((0,), (0,)), ((), ())), preferred_element_type=jnp.float32)
    d_tail = d_pos[:, None] * query_bf
    d_head = conj_mul(d_query, rel_rows)
    d_rel = conj_mul(d_query, head_rows)
    return d_head, d_tail, d_negrows, d_rel, round_loss


def solution(mesh):
    group_size = mesh.shape["ent"]
    row_spec = P(("sweep", "ent"))
    table_spec = P(("sweep", "ent"), None)
    edge_spec = P(("sweep", "ent"), None, None)
    rel_spec = P("sweep", None)
    racc_spec = P("sweep")

    def device_step(ent_table, ent_accum, rel_table, rel_accum, head_idx, tail_idx, rel_idx, edge_mask, neg_idx):
        part_rows = ent_table.shape[0]
        num_rels = rel_table.shape[0]
        cur_table, cur_accum, cur_rel, rel_acc = ent_table, ent_accum, rel_table, rel_accum
        loss_list = []
        for shift in range(group_size):
            heads_now = head_idx[0, shift]
            tails_now = tail_idx[0, shift]
            rels_now = rel_idx[0, shift]
            negs_now = neg_idx[0, shift]
            own_bf = cur_table.astype(jnp.bfloat16)
            if shift == 0:
                tail_part = own_bf
            else:
                tail_part = lax.ppermute(own_bf, "ent", perm=[(sender, (sender - shift) % group_size) for sender in range(group_size)])
            head_rows = jnp.take(cur_table, heads_now, axis=0)
            rel_rows = jnp.take(cur_rel, rels_now, axis=0)
            tail_rows = jnp.take(tail_part, tails_now, axis=0)
            neg_rows = jnp.take(tail_part, negs_now, axis=0)
            d_head, d_tail, d_negrows, d_rel, round_loss = bucket_grads(head_rows, rel_rows, tail_rows, neg_rows, edge_mask[0, shift])
            head_grad = jax.ops.segment_sum(d_head, heads_now, num_segments=part_rows)
            tail_grad = jax.ops.segment_sum(jnp.concatenate([d_tail, d_negrows], axis=0), jnp.concatenate([tails_now, negs_now]), num_segments=part_rows)
            if shift == 0:
                row_grad = head_grad + tail_grad
            else:
                row_grad = head_grad + lax.ppermute(tail_grad, "ent", perm=[(sender, (sender + shift) % group_size) for sender in range(group_size)])
            rel_grad = lax.psum(jax.ops.segment_sum(d_rel, rels_now, num_segments=num_rels), "ent")
            cur_table, cur_accum = adagrad(cur_table, cur_accum, row_grad, LR_ENT)
            cur_rel, rel_acc = adagrad(cur_rel, rel_acc, rel_grad, LR_REL)
            loss_list.append(round_loss)
        return cur_table, cur_accum, cur_rel, rel_acc, jnp.stack(loss_list)[None, :]

    return jax.shard_map(device_step, mesh=mesh, in_specs=(table_spec, row_spec, rel_spec, racc_spec, edge_spec, edge_spec, edge_spec, edge_spec, edge_spec), out_specs=(table_spec, row_spec, rel_spec, racc_spec, P(("sweep", "ent"), None)), check_vma=False)
```

profile of v0, /device:TPU:112, one launch (start us, length us, event | category | flops | bytes accessed | tf_op | source)
XLA Modules:
  0.0 1804.8 jit_solution(3891487513400377261)
XLA Ops:
  15.3 10.8 gather_fusion
  75.1 10.0 convolution_add_fusion.7
  100.4 14.1 scatter_custom_fusion
  114.5 25.0 %scatter_custom_fusion.1 = f32[4096,200]{1,0:T(8,128)} fusion(s32[4096]{0:T(1024)} %pad_add_fusion, f32[4096,200]{1,0:T(8,128)} %copy.100, f32[]{:T(128)} %constant.76.clone.1), kind=kCustom, calls=%fused_computation.150 | custom fusion | flops 819200 | bytes 3277312 | tf_op jit(solution)/shard_map/scatter-add | solution.py:79
  178.8 12.0 scatter_custom_fusion.2
  190.7 24.1 %psum.56 = f32[11,200]{1,0:T(8,128)S(1)} all-reduce(f32[11,200]{1,0:T(8,128)S(1)} %scatter_custom_fusion.2), channel_id=1, replica_groups=mesh['sweep'=2,'ent'=8] {'ent'}, use_global_device_ids=true, to_apply=%region_6.10 | all-reduce | flops 2200 | bytes 17600 | tf_op jit(solution)/shard_map/psum | solution.py:84
  289.3 25.4 %scatter_custom_fusion.3 = f32[4096,200]{1,0:T(8,128)} fusion(s32[4096]{0:T(1024)} %pad_add_fusion.1, f32[4096,200]{1,0:T(8,128)} %copy.109, f32[]{:T(128)} %constant.76.clone.1), kind=kCustom, calls=%fused_computation.148 | custom fusion | flops 819200 | bytes 3277312 | tf_op jit(solution)/shard_map/scatter-add | solution.py:79
  332.3 12.0 scatter_custom_fusion.5
  347.4 30.1 %psum.57 = f32[11,200]{1,0:T(8,128)S(1)} all-reduce(f32[11,200]{1,0:T(8,128)S(1)} %scatter_custom_fusion.5), channel_id=1, replica_groups=mesh['sweep'=2,'ent'=8] {'ent'}, use_global_device_ids=true, to_apply=%region_14.18 | all-reduce | flops 2200 | bytes 17600 | tf_op jit(solution)/shard_map/psum | solution.py:84
  382.9 15.6 scatter_fusion
  418.9 11.4 gather_fusion.8
  433.5 10.4 collective-permute-done.2
  447.1 9.1 gather_fusion.10
  494.4 25.2 %scatter_custom_fusion.6 = f32[4096,200]{1,0:T(8,128)} fusion(s32[4096]{0:T(1024)} %pad_add_fusion.2, f32[4096,200]{1,0:T(8,128)} %copy.120, f32[]{:T(128)} %constant.76.clone.1), kind=kCustom, calls=%fused_computation.146 | custom fusion | flops 819200 | bytes 3277312 | tf_op jit(solution)/shard_map/scatter-add | solution.py:79
  537.2 12.0 scatter_custom_fusion.8
  552.4 63.0 %psum.58 = f32[11,200]{1,0:T(8,128)S(1)} all-reduce(f32[11,200]{1,0:T(8,128)S(1)} %scatter_custom_fusion.8), channel_id=1, replica_groups=mesh['sweep'=2,'ent'=8] {'ent'}, use_global_device_ids=true, to_apply=%region_22.26 | all-reduce | flops 2200 | bytes 17600 | tf_op jit(solution)/shard_map/psum | solution.py:84
  620.7 15.6 scatter_fusion.1
  657.0 11.4 gather_fusion.12
  671.6 12.3 collective-permute-done.4
  734.3 25.2 %scatter_custom_fusion.9 = f32[4096,200]{1,0:T(8,128)} fusion(s32[4096]{0:T(1024)} %pad_add_fusion.3, f32[4096,200]{1,0:T(8,128)} %copy.131, f32[]{:T(128)} %constant.76.clone.1), kind=kCustom, calls=%fused_computation.144 | custom fusion | flops 819200 | bytes 3277312 | tf_op jit(solution)/shard_map/scatter-add | solution.py:79
  777.1 12.0 scatter_custom_fusion.11
  792.3 62.0 %psum.59 = f32[11,200]{1,0:T(8,128)S(1)} all-reduce(f32[11,200]{1,0:T(8,128)S(1)} %scatter_custom_fusion.11), channel_id=1, replica_groups=mesh['sweep'=2,'ent'=8] {'ent'}, use_global_device_ids=true, to_apply=%region_30.34 | all-reduce | flops 2200 | bytes 17600 | tf_op jit(solution)/shard_map/psum | solution.py:84
  859.6 15.6 scatter_fusion.2
  895.8 11.4 gather_fusion.16
  910.4 13.4 collective-permute-done.6
  927.1 9.1 gather_fusion.18
  974.3 25.2 %scatter_custom_fusion.12 = f32[4096,200]{1,0:T(8,128)} fusion(s32[4096]{0:T(1024)} %pad_add_fusion.4, f32[4096,200]{1,0:T(8,128)} %copy.142, f32[]{:T(128)} %constant.76.clone.1), kind=kCustom, calls=%fused_computation.142 | custom fusion | flops 819200 | bytes 3277312 | tf_op jit(solution)/shard_map/scatter-add | solution.py:79
  1016.7 12.0 scatter_custom_fusion.14
  1031.9 62.6 %psum.60 = f32[11,200]{1,0:T(8,128)S(1)} all-reduce(f32[11,200]{1,0:T(8,128)S(1)} %scatter_custom_fusion.14), channel_id=1, replica_groups=mesh['sweep'=2,'ent'=8] {'ent'}, use_global_device_ids=true, to_apply=%region_38.42 | all-reduce | flops 2200 | bytes 17600 | tf_op jit(solution)/shard_map/psum | solution.py:84
  1099.8 15.6 scatter_fusion.3
  1136.1 11.4 gather_fusion.20
  1150.6 12.9 collective-permute-done.8
  1213.9 25.2 %scatter_custom_fusion.15 = f32[4096,200]{1,0:T(8,128)} fusion(s32[4096]{0:T(1024)} %pad_add_fusion.5, f32[4096,200]{1,0:T(8,128)} %copy.153, f32[]{:T(128)} %constant.76.clone.1), kind=kCustom, calls=%fused_computation.140 | custom fusion | flops 819200 | bytes 3277312 | tf_op jit(solution)/shard_map/scatter-add | solution.py:79
  1255.0 12.0 scatter_custom_fusion.17
  1270.2 61.0 %psum.61 = f32[11,200]{1,0:T(8,128)S(1)} all-reduce(f32[11,200]{1,0:T(8,128)S(1)} %scatter_custom_fusion.17), channel_id=1, replica_groups=mesh['sweep'=2,'ent'=8] {'ent'}, use_global_device_ids=true, to_apply=%region_46.50 | all-reduce | flops 2200 | bytes 17600 | tf_op jit(solution)/shard_map/psum | solution.py:84
  1336.5 15.6 scatter_fusion.4
  1372.7 11.4 gather_fusion.24
  1387.3 11.2 collective-permute-done.10
  1401.7 9.1 gather_fusion.26
  1448.9 25.2 %scatter_custom_fusion.18 = f32[4096,200]{1,0:T(8,128)} fusion(s32[4096]{0:T(1024)} %pad_add_fusion.6, f32[4096,200]{1,0:T(8,128)} %copy.164, f32[]{:T(128)} %constant.76.clone.1), kind=kCustom, calls=%fused_computation.138 | custom fusion | flops 819200 | bytes 3277312 | tf_op jit(solution)/shard_map/scatter-add | solution.py:79
  1491.7 12.0 scatter_custom_fusion.20
  1506.8 65.5 %psum.62 = f32[11,200]{1,0:T(8,128)S(1)} all-reduce(f32[11,200]{1,0:T(8,128)S(1)} %scatter_custom_fusion.20), channel_id=1, replica_groups=mesh['sweep'=2,'ent'=8] {'ent'}, use_global_device_ids=true, to_apply=%region_54.58 | all-reduce | flops 2200 | bytes 17600 | tf_op jit(solution)/shard_map/psum | solution.py:84
  1577.6 15.6 scatter_fusion.5
  1613.6 11.4 gather_fusion.28
  1678.6 25.4 %scatter_custom_fusion.21 = f32[4096,200]{1,0:T(8,128)} fusion(s32[4096]{0:T(1024)} %pad_add_fusion.7, f32[4096,200]{1,0:T(8,128)} %copy.175, f32[]{:T(128)} %constant.76.clone.1), kind=kCustom, calls=%fused_computation.136 | custom fusion | flops 819200 | bytes 3277312 | tf_op jit(solution)/shard_map/scatter-add | solution.py:79
  1727.9 12.0 scatter_custom_fusion.23
  1743.7 26.0 %psum.63 = f32[11,200]{1,0:T(8,128)S(1)} all-reduce(f32[11,200]{1,0:T(8,128)S(1)} %scatter_custom_fusion.23), channel_id=1, replica_groups=mesh['sweep'=2,'ent'=8] {'ent'}, use_global_device_ids=true, to_apply=%region_62.66 | all-reduce | flops 2200 | bytes 17600 | tf_op jit(solution)/shard_map/psum | solution.py:84
  1776.2 15.6 scatter_fusion.6
  (687 shorter events, 804.8 us)
Async XLA Ops:
  2.5 158.8 %copy-start.94 = (s32[1,1,2048]{2,1,0:T(1,128)}, s32[1,1,2048]{2,1,0:T(1,128)S(1)}, u32[]{:S(2)}) copy-start(s32[1,1,2048]{2,1,0:T(1,128)S(1)} %get-tuple-element.152) | copy-start | bytes 24580
  2.5 164.2 %copy-start.93 = (s32[1,1,2048]{2,1,0:T(1,128)}, s32[1,1,2048]{2,1,0:T(1,128)S(1)}, u32[]{:S(2)}) copy-start(s32[1,1,2048]{2,1,0:T(1,128)S(1)} %get-tuple-element.151) | copy-start | bytes 24580
  2.5 318.2 %copy-start.92 = (s32[1,1,2048]{2,1,0:T(1,128)}, s32[1,1,2048]{2,1,0:T(1,128)S(1)}, u32[]{:S(2)}) copy-start(s32[1,1,2048]{2,1,0:T(1,128)S(1)} %get-tuple-element.150) | copy-start | bytes 24580
  4.5 153.3 %copy-start.76 = (s32[1,1,2048]{2,1,0:T(1,128)}, s32[1,1,2048]{2,1,0:T(1,128)S(1)}, u32[]{:S(2)}) copy-start(s32[1,1,2048]{2,1,0:T(1,128)S(1)} %get-tuple-element.145) | copy-start | bytes 24580
  4.5 158.7 %copy-start.74 = (s32[1,1,2048]{2,1,0:T(1,128)}, s32[1,1,2048]{2,1,0:T(1,128)S(1)}, u32[]{:S(2)}) copy-start(s32[1,1,2048]{2,1,0:T(1,128)S(1)} %get-tuple-element.144) | copy-start | bytes 24580
  4.5 164.1 %copy-start.72 = (s32[1,1,2048]{2,1,0:T(1,128)}, s32[1,1,2048]{2,1,0:T(1,128)S(1)}, u32[]{:S(2)}) copy-start(s32[1,1,2048]{2,1,0:T(1,128)S(1)} %get-tuple-element.143) | copy-start | bytes 24580
  4.5 316.9 %copy-start.70 = (s32[1,1,2048]{2,1,0:T(1,128)}, s32[1,1,2048]{2,1,0:T(1,128)S(1)}, u32[]{:S(2)}) copy-start(s32[1,1,2048]{2,1,0:T(1,128)S(1)} %get-tuple-element.142) | copy-start | bytes 24580
  6.4 166.9 %copy-start.86 = (s32[1,1,2048]{2,1,0:T(1,128)}, s32[1,1,2048]{2,1,0:T(1,128)S(1)}, u32[]{:S(2)}) copy-start(s32[1,1,2048]{2,1,0:T(1,128)S(1)} %get-tuple-element.158) | copy-start | bytes 24580
  6.4 168.6 %copy-start.82 = (s32[1,1,2048]{2,1,0:T(1,128)}, s32[1,1,2048]{2,1,0:T(1,128)S(1)}, u32[]{:S(2)}) copy-start(s32[1,1,2048]{2,1,0:T(1,128)S(1)} %get-tuple-element.164) | copy-start | bytes 24580
  6.4 228.7 %copy-start.78 = (s32[1,1,2048]{2,1,0:T(1,128)}, s32[1,1,2048]{2,1,0:T(1,128)S(1)}, u32[]{:S(2)}) copy-start(s32[1,1,2048]{2,1,0:T(1,128)S(1)} %get-tuple-element.157) | copy-start | bytes 24580
  7.7 165.6 %copy-start.88 = (s32[1,1,2048]{2,1,0:T(1,128)}, s32[1,1,2048]{2,1,0:T(1,128)S(1)}, u32[]{:S(2)}) copy-start(s32[1,1,2048]{2,1,0:T(1,128)S(1)} %get-tuple-element.166) | copy-start | bytes 24580
  7.7 167.3 %copy-start.84 = (s32[1,1,2048]{2,1,0:T(1,128)}, s32[1,1,2048]{2,1,0:T(1,128)S(1)}, u32[]{:S(2)}) copy-start(s32[1,1,2048]{2,1,0:T(1,128)S(1)} %get-tuple-element.172) | copy-start | bytes 24580
  7.7 227.4 %copy-start.80 = (s32[1,1,2048]{2,1,0:T(1,128)}, s32[1,1,2048]{2,1,0:T(1,128)S(1)}, u32[]{:S(2)}) copy-start(s32[1,1,2048]{2,1,0:T(1,128)S(1)} %get-tuple-element.165) | copy-start | bytes 24580
  75.1 11.2 copy-start.10
  149.7 26.0 %copy-start.54 = (f32[2048,100]{0,1:T(8,128)S(1)}, f32[2048,100]{0,1:T(8,128)}, u32[]{:S(2)}) copy-start(f32[2048,100]{0,1:T(8,128)} %get-tuple-element.111) | copy-start | bytes 2457604
  152.4 86.6 %collective-permute-start = (bf16[4096,200]{0,1:T(8,128)(2,1)}, bf16[4096,200]{0,1:T(8,128)(2,1)}, u32[]{:S(2)}, u32[]{:S(2)}) collective-permute-start(bf16[4096,200]{0,1:T(8,128)(2,1)} %copy.105), channel_id=1, source_target_pairs={{0,7},{1,0},{2,1},{3,2},{4,3},{5,4},{6,5},{7,6},{8,15},{9,8},{10,9... | collective-permute-start | bytes 4915208 | tf_op jit(solution)/shard_map/ppermute | solution.py:72
  155.9 106.5 %copy-start.136 = (pred[2048]{0:T(1024)(128)(4,1)}, pred[2048]{0:T(1024)(128)(4,1)S(1)}, u32[]{:S(2)}) copy-start(pred[2048]{0:T(1024)(128)(4,1)S(1)} %compare_and_fusion.25) | copy-start | bytes 6148
  155.9 108.0 %copy-start.138 = (pred[2048]{0:T(1024)(128)(4,1)}, pred[2048]{0:T(1024)(128)(4,1)S(1)}, u32[]{:S(2)}) copy-start(pred[2048]{0:T(1024)(128)(4,1)S(1)} %compare_and_fusion.24) | copy-start | bytes 6148
  177.0 38.0 %copy-start.151 = (f32[11]{0:T(128)S(1)}, f32[11]{0:T(128)}, u32[]{:S(2)}) copy-start(f32[11]{0:T(128)} %param.18) | copy-start | bytes 136
  320.2 57.4 %collective-permute-start.1 = (f32[4096,200]{0,1:T(8,128)}, f32[4096,200]{0,1:T(8,128)}, u32[]{:S(2)}, u32[]{:S(2)}) collective-permute-start(f32[4096,200]{0,1:T(8,128)} %copy.110), channel_id=1, source_target_pairs={{0,1},{1,2},{2,3},{3,4},{4,5},{5,6},{6,7},{7,0},{8,9},{9,10},{10,1... | collective-permute-start | bytes 9830408 | tf_op jit(solution)/shard_map/ppermute | solution.py:83
  408.8 35.1 %collective-permute-start.2 = (bf16[4096,200]{0,1:T(8,128)(2,1)}, bf16[4096,200]{0,1:T(8,128)(2,1)}, u32[]{:S(2)}, u32[]{:S(2)}) collective-permute-start(bf16[4096,200]{0,1:T(8,128)(2,1)} %copy.116), channel_id=1, source_target_pairs={{0,6},{1,7},{2,0},{3,1},{4,2},{5,3},{6,4},{7,5},{8,14},{9,15},{10,... | collective-permute-start | bytes 4915208 | tf_op jit(solution)/shard_map/ppermute | solution.py:72
  418.9 13.4 copy-start.17
  433.5 13.6 copy-start.124
  447.1 11.3 copy-start.123
  525.1 90.5 %collective-permute-start.3 = (f32[4096,200]{0,1:T(8,128)}, f32[4096,200]{0,1:T(8,128)}, u32[]{:S(2)}, u32[]{:S(2)}) collective-permute-start(f32[4096,200]{0,1:T(8,128)} %copy.121), channel_id=1, source_target_pairs={{0,2},{1,3},{2,4},{3,5},{4,6},{5,7},{6,0},{7,1},{8,10},{9,11},{10,... | collective-permute-start | bytes 9830408 | tf_op jit(solution)/shard_map/ppermute | solution.py:83
  647.0 37.0 %collective-permute-start.4 = (bf16[4096,200]{0,1:T(8,128)(2,1)}, bf16[4096,200]{0,1:T(8,128)(2,1)}, u32[]{:S(2)}, u32[]{:S(2)}) collective-permute-start(bf16[4096,200]{0,1:T(8,128)(2,1)} %copy.127), channel_id=1, source_target_pairs={{0,5},{1,6},{2,7},{3,0},{4,1},{5,2},{6,3},{7,4},{8,13},{9,14},{10,... | collective-permute-start | bytes 4915208 | tf_op jit(solution)/shard_map/ppermute | solution.py:72
  657.0 13.4 copy-start.23
  671.6 15.5 copy-start.122
  687.1 11.3 copy-start.121
  765.0 89.4 %collective-permute-start.5 = (f32[4096,200]{0,1:T(8,128)}, f32[4096,200]{0,1:T(8,128)}, u32[]{:S(2)}, u32[]{:S(2)}) collective-permute-start(f32[4096,200]{0,1:T(8,128)} %copy.132), channel_id=1, source_target_pairs={{0,3},{1,4},{2,5},{3,6},{4,7},{5,0},{6,1},{7,2},{8,11},{9,12},{10,... | collective-permute-start | bytes 9830408 | tf_op jit(solution)/shard_map/ppermute | solution.py:83
  885.8 38.1 %collective-permute-start.6 = (bf16[4096,200]{0,1:T(8,128)(2,1)}, bf16[4096,200]{0,1:T(8,128)(2,1)}, u32[]{:S(2)}, u32[]{:S(2)}) collective-permute-start(bf16[4096,200]{0,1:T(8,128)(2,1)} %copy.138), channel_id=1, source_target_pairs={{0,4},{1,5},{2,6},{3,7},{4,0},{5,1},{6,2},{7,3},{8,12},{9,13},{10,... | collective-permute-start | bytes 4915208 | tf_op jit(solution)/shard_map/ppermute | solution.py:72
  895.8 13.5 copy-start.15
  910.4 16.6 copy-start.118
  927.0 11.3 copy-start.117
  1005.0 89.6 %collective-permute-start.7 = (f32[4096,200]{0,1:T(8,128)}, f32[4096,200]{0,1:T(8,128)}, u32[]{:S(2)}, u32[]{:S(2)}) collective-permute-start(f32[4096,200]{0,1:T(8,128)} %copy.143), channel_id=1, source_target_pairs={{0,4},{1,5},{2,6},{3,7},{4,0},{5,1},{6,2},{7,3},{8,12},{9,13},{10,... | collective-permute-start | bytes 9830408 | tf_op jit(solution)/shard_map/ppermute | solution.py:83
  1126.0 37.6 %collective-permute-start.8 = (bf16[4096,200]{0,1:T(8,128)(2,1)}, bf16[4096,200]{0,1:T(8,128)(2,1)}, u32[]{:S(2)}, u32[]{:S(2)}) collective-permute-start(bf16[4096,200]{0,1:T(8,128)(2,1)} %copy.149), channel_id=1, source_target_pairs={{0,3},{1,4},{2,5},{3,6},{4,7},{5,0},{6,1},{7,2},{8,11},{9,12},{10,... | collective-permute-start | bytes 4915208 | tf_op jit(solution)/shard_map/ppermute | solution.py:72
  1136.0 13.4 copy-start.21
  1150.6 16.1 copy-start.120
  1166.7 11.3 copy-start.119
  1244.6 86.7 %collective-permute-start.9 = (f32[4096,200]{0,1:T(8,128)}, f32[4096,200]{0,1:T(8,128)}, u32[]{:S(2)}, u32[]{:S(2)}) collective-permute-start(f32[4096,200]{0,1:T(8,128)} %copy.154), channel_id=1, source_target_pairs={{0,5},{1,6},{2,7},{3,0},{4,1},{5,2},{6,3},{7,4},{8,13},{9,14},{10,... | collective-permute-start | bytes 9830408 | tf_op jit(solution)/shard_map/ppermute | solution.py:83
  1362.7 35.9 %collective-permute-start.10 = (bf16[4096,200]{0,1:T(8,128)(2,1)}, bf16[4096,200]{0,1:T(8,128)(2,1)}, u32[]{:S(2)}, u32[]{:S(2)}) collective-permute-start(bf16[4096,200]{0,1:T(8,128)(2,1)} %copy.160), channel_id=1, source_target_pairs={{0,2},{1,3},{2,4},{3,5},{4,6},{5,7},{6,0},{7,1},{8,10},{9,11},{10,... | collective-permute-start | bytes 4915208 | tf_op jit(solution)/shard_map/ppermute | solution.py:72
  1372.7 13.5 copy-start.19
  1479.6 92.9 %collective-permute-start.11 = (f32[4096,200]{0,1:T(8,128)}, f32[4096,200]{0,1:T(8,128)}, u32[]{:S(2)}, u32[]{:S(2)}) collective-permute-start(f32[4096,200]{0,1:T(8,128)} %copy.165), channel_id=1, source_target_pairs={{0,6},{1,7},{2,0},{3,1},{4,2},{5,3},{6,4},{7,5},{8,14},{9,15},{10,... | collective-permute-start | bytes 9830408 | tf_op jit(solution)/shard_map/ppermute | solution.py:83
  1603.6 24.7 %collective-permute-start.12 = (bf16[4096,200]{0,1:T(8,128)(2,1)}, bf16[4096,200]{0,1:T(8,128)(2,1)}, u32[]{:S(2)}, u32[]{:S(2)}) collective-permute-start(bf16[4096,200]{0,1:T(8,128)(2,1)} %copy.171), channel_id=1, source_target_pairs={{0,1},{1,2},{2,3},{3,4},{4,5},{5,6},{6,7},{7,0},{8,9},{9,10},{10,1... | collective-permute-start | bytes 4915208 | tf_op jit(solution)/shard_map/ppermute | solution.py:72
  1613.6 13.4 copy-start.11
  1704.0 13.5 copy-start.41
  1704.0 13.5 copy-start.55
  1709.5 61.5 %collective-permute-start.13 = (f32[4096,200]{0,1:T(8,128)}, f32[4096,200]{0,1:T(8,128)}, u32[]{:S(2)}, u32[]{:S(2)}) collective-permute-start(f32[4096,200]{0,1:T(8,128)} %copy.176), channel_id=1, source_target_pairs={{0,7},{1,0},{2,1},{3,2},{4,3},{5,4},{6,5},{7,6},{8,15},{9,8},{10,9... | collective-permute-start | bytes 9830408 | tf_op jit(solution)/shard_map/ppermute | solution.py:83
  (118 other events, 572.5 us)
where the time goes:
time: 1820 us; the launch traced here: 1800 us
  other arithmetic  660 us (36%)
  local copies, waits for them, and re-layouts  534 us (29%)
  blocking collectives  394 us (22%)
  matrix products  139 us (8%)
  waiting for transfers between devices  60.4 us (3%)
    psum x8, blocking collectives, device_step(): lax.psum(jax.ops.segment_sum(d_rel, rels_now, num_segments=num_rels), 'ent')  394 us
    scatter-add x8, other arithmetic, device_step(): jax.ops.segment_sum(jnp.concatenate([d_tail, d_negrows], axis=0), jnp.con...  202 us
    scatter-add x8, other arithmetic, device_step(): head_grad = jax.ops.segment_sum(d_head, heads_now, num_segments=part_rows)  123 us
    gather x16, local copies, waits for them, and re-layouts, device_step(): head_rows = jnp.take(cur_table, heads_now, axis=0)  104 us
    scatter-add x8, other arithmetic, device_step(): jax.ops.segment_sum(d_rel, rels_now, num_segments=num_rels)  95.7 us
    gather x16, local copies, waits for them, and re-layouts, device_step(): tail_rows = jnp.take(tail_part, tails_now, axis=0)  87.5 us
    gather x8, local copies, waits for them, and re-layouts, device_step(): neg_rows = jnp.take(tail_part, negs_now, axis=0)  70.3 us
    gather x16, local copies, waits for them, and re-layouts, device_step(): rel_rows = jnp.take(cur_rel, rels_now, axis=0)  69.8 us
  transfers between devices with their start and end apart: 14, of which 5 were waited for; matrix products, arithmetic and copies ran while one was open for 21% of the time, Pallas kernels for 0%

commit v1 on v0

v1 whole, which is shorter than its diff:
```python
import functools

import jax
import jax.numpy as jnp
from jax import lax
from jax.experimental import pallas as pl
from jax.experimental.pallas import tpu as pltpu
from jax.sharding import PartitionSpec as P

LR_ENT = 0.03
LR_REL = 0.05
ADA_EPS = 1e-10
LANES = 128
MIB = 1024 * 1024
F32 = jnp.float32
BF16 = jnp.bfloat16
MESH = pl.DeviceIdType.MESH
VMEM = pl.BlockSpec(memory_space=pltpu.VMEM)
SMEM = pl.BlockSpec(memory_space=pltpu.SMEM)


def even(start, size):
    return pl.ds(start, size, stride=2)


def row_pair(index):
    return pl.ds(pl.multiple_of(index, 2), 2)


def transpose_row(row, width):
    return jnp.transpose(jnp.broadcast_to(row, (LANES, width)))


def gather_rows(count, streams, unroll=8):
    def body(step, carry):
        for sub in range(unroll):
            slot = step * unroll + sub
            for index_of, src, dst in streams:
                dst[row_pair(2 * slot), :] = src[row_pair(index_of(slot)), :]
        return carry

    lax.fori_loop(0, count // unroll, body, 0)


def scatter_rows(count, streams, unroll=4):
    def body(step, carry):
        for sub in range(unroll):
            slot = step * unroll + sub
            for index_of, src, table in streams:
                where = row_pair(index_of(slot))
                table[where, :] = table[where, :] + src[row_pair(2 * slot), :]
        return carry

    lax.fori_loop(0, count // unroll, body, 0)


def rel_exchange(group, part_ref, recv_ref, send_sem, recv_sem):
    me = lax.axis_index("ent")
    barrier = pltpu.get_barrier_semaphore()
    for off in range(1, group):
        pl.semaphore_signal(barrier, inc=1, device_id={"ent": lax.rem(me + off, group)}, device_id_type=MESH)
    pl.semaphore_wait(barrier, group - 1)
    copies = []
    for off in range(1, group):
        copy = pltpu.make_async_remote_copy(
            src_ref=part_ref,
            dst_ref=recv_ref.at[off],
            send_sem=send_sem.at[off],
            recv_sem=recv_sem.at[off],
            device_id={"ent": lax.rem(me + off, group)},
            device_id_type=MESH,
        )
        copy.start()
        copies.append(copy)

    def wait():
        for copy in copies:
            copy.wait()
        total = None
        for dev in range(group):
            off = lax.rem(me - dev + group, group)
            term = jnp.where(off == 0, part_ref[...], recv_ref[off])
            total = term if total is None else total + term
        return total

    return wait


def rel_update(total, rel, racc, dim):
    acc = racc + jnp.sum(total * total, axis=1, keepdims=True) * (1.0 / dim)
    scale = LR_REL * lax.rsqrt(acc + ADA_EPS)
    return rel - total * scale[:, :1], acc


def query_kernel(shift, ent, rel, own_idx, tail_idx, q_out, neg_out, tail_out, head_out, relrow_out, rel_pairs, buf_neg, buf_tail):
    count = q_out.shape[0]
    rels = rel.shape[0]
    gather_rows(count, [
        (lambda b: own_idx[shift, 0, b], ent, head_out),
        (lambda b: tail_idx[0, b], ent, buf_tail),
        (lambda b: tail_idx[1, b], ent, buf_neg),
    ])
    rel_pairs[even(0, rels), :] = rel[:, :LANES]
    rel_pairs[even(1, rels), :] = rel[:, LANES:]
    gather_rows(count, [(lambda b: own_idx[shift, 1, b], rel_pairs, relrow_out)])
    block = 128

    def body(step, carry):
        base = pl.multiple_of(step * block, block)
        rows = pl.ds(base, block)
        for src, dst in ((buf_neg, neg_out), (buf_tail, tail_out)):
            dst[rows, :LANES] = src[even(2 * base, block), :].astype(BF16)
            dst[rows, LANES:] = src[even(2 * base + 1, block), :].astype(BF16)
        head_re, head_im = head_out[even(2 * base, block), :], head_out[even(2 * base + 1, block), :]
        rel_re, rel_im = relrow_out[even(2 * base, block), :], relrow_out[even(2 * base + 1, block), :]
        q_out[rows, :LANES] = (head_re * rel_re - head_im * rel_im).astype(BF16)
        q_out[rows, LANES:] = (head_re * rel_im + head_im * rel_re).astype(BF16)
        return carry

    lax.fori_loop(0, count // block, body, 0)


def score_kernel(half, q, neg, tail, idx, dq_out, dneg_out, dtail_out, neg_t, score, attn):
    count, negs = q.shape[0], neg.shape[0]
    width = 256
    keep = dq_out.shape[0] // 2
    block = 128

    def flip(step, carry):
        cols = pl.ds(pl.multiple_of(step * width, width), width)
        neg_t[:, cols] = jnp.transpose(neg[cols, :].astype(F32)).astype(BF16)
        return carry

    lax.fori_loop(0, negs // width, flip, 0)

    def chunk(step, carry):
        base = pl.multiple_of(step * width, width)
        cols = pl.ds(base, width)
        q_now = q[cols, :]
        q_f32 = q_now.astype(F32)
        tail_f32 = tail[cols, :].astype(F32)
        score[...] = lax.dot_general(neg[...], q_now, (((1,), (1,)), ((), ())), preferred_element_type=F32)
        pos_col = jnp.sum(q_f32 * tail_f32, axis=1, keepdims=True)
        pos = jnp.transpose(jnp.broadcast_to(pos_col, (width, LANES)))[0:1, :]

        def top(k, best):
            part = score[pl.ds(pl.multiple_of(k * block, block), block), :]
            return jnp.maximum(best, jnp.max(part.reshape(block // 8, 8, width), axis=0))

        best = lax.fori_loop(0, negs // block, top, jnp.broadcast_to(pos, (8, width)))
        peak = jnp.max(best, axis=0, keepdims=True)

        def expo(k, acc):
            rows = pl.ds(pl.multiple_of(k * block, block), block)
            part = jnp.exp(score[rows, :] - peak)
            score[rows, :] = part
            return acc + jnp.sum(part.reshape(block // 8, 8, width), axis=0)

        acc = lax.fori_loop(0, negs // block, expo, jnp.zeros((8, width), F32))
        pos_exp = jnp.exp(pos - peak)
        norm = jnp.sum(acc, axis=0, keepdims=True) + pos_exp
        weight = idx[2:3, cols].astype(F32)
        inv = 1.0 / norm
        loss = weight * (peak + jnp.log(norm) - pos)
        d_pos = weight * (pos_exp * inv - 1.0)
        scale = weight * inv

        def scaled(k, carry):
            rows = pl.ds(pl.multiple_of(k * block, block), block)
            attn[rows, cols] = (score[rows, :] * scale).astype(BF16)
            return carry

        lax.fori_loop(0, negs // block, scaled, 0)
        d_q = jnp.dot(neg_t[...], attn[:, cols], preferred_element_type=F32) + d_pos * jnp.transpose(tail_f32)
        line = lax.broadcasted_iota(jnp.int32, (keep, width), 0)
        dq_out[:keep, cols] = d_q[:keep] + jnp.where(line == half, loss, 0.0)
        dq_out[keep:, cols] = d_q[LANES:LANES + keep]
        d_col = transpose_row(d_pos, width)
        dtail_out[even(2 * base, width), :] = d_col * q_f32[:, :LANES]
        dtail_out[even(2 * base + 1, width), :] = d_col * q_f32[:, LANES:]
        return carry

    lax.fori_loop(0, count // width, chunk, 0)
    rows_per = 512

    def back(step, carry):
        base = pl.multiple_of(step * rows_per, rows_per)
        got = jnp.dot(attn[pl.ds(base, rows_per), :], q[...], preferred_element_type=F32)
        dneg_out[even(2 * base, rows_per), :] = got[:, :LANES]
        dneg_out[even(2 * base + 1, rows_per), :] = got[:, LANES:]
        return carry

    lax.fori_loop(0, negs // rows_per, back, 0)


def split3(value):
    first = value.astype(BF16)
    rest = value - first.astype(F32)
    second = rest.astype(BF16)
    return first, second, (rest - second.astype(F32)).astype(BF16)


def update_kernel(dim, shift, ent, acc, dneg, dtail, dq, head, relrow, own_idx, own_vec, tail_idx, ent_out, acc_out, part_out, loss_out,
                  table_a, table_b, table_c, dhead):
    count = dhead.shape[0] // 2
    half = dim // 2
    keep = dq.shape[0] // 2
    rows_all = ent.shape[0]
    rels = part_out.shape[0]
    block = 128

    def zero(step, carry):
        rows = pl.ds(pl.multiple_of(step * 256, 256), 256)
        for table in (table_a, table_b, table_c):
            table[rows, :] = jnp.zeros((256, LANES), F32)
        return carry

    lax.fori_loop(0, rows_all // 256, zero, 0)
    loss_out[...] = jnp.broadcast_to(jnp.sum(dq[half:half + 1, :]) * (1.0 / count), loss_out.shape)
    part_out[...] = jnp.zeros(part_out.shape, F32)

    def heads(step, carry):
        base = pl.multiple_of(step * block, block)
        cols = pl.ds(base, block)
        line = lax.broadcasted_iota(jnp.int32, (keep, block), 0)
        pad = jnp.zeros((LANES - keep, block), F32)
        d_re = jnp.transpose(jnp.concatenate([jnp.where(line < half, dq[:keep, cols], 0.0), pad], axis=0))
        d_im = jnp.transpose(jnp.concatenate([dq[keep:, cols], pad], axis=0))
        rel_re, rel_im = relrow[even(2 * base, block), :], relrow[even(2 * base + 1, block), :]
        dhead[even(2 * base, block), :] = d_re * rel_re + d_im * rel_im
        dhead[even(2 * base + 1, block), :] = d_im * rel_re - d_re * rel_im
        head_re, head_im = head[even(2 * base, block), :], head[even(2 * base + 1, block), :]
        drel = jnp.concatenate([d_re * head_re + d_im * head_im, d_im * head_re - d_re * head_im], axis=1)
        pick = lax.broadcasted_iota(jnp.int32, (rels, block), 0) == own_vec[shift, 1:2, cols]
        hot = jnp.where(pick, 1.0, 0.0).astype(BF16)
        total = part_out[...]
        for piece in split3(drel):
            total = total + jnp.dot(hot, piece, preferred_element_type=F32)
        part_out[...] = total
        return carry

    lax.fori_loop(0, count // block, heads, 0)
    scatter_rows(count, [
        (lambda b: own_idx[shift, 0, b], dhead, table_a),
        (lambda b: tail_idx[0, b], dtail, table_b),
        (lambda b: tail_idx[1, b], dneg, table_c),
    ])

    def step_rows(step, carry):
        base = pl.multiple_of(step * block, block)
        rows = pl.ds(base, block)
        lo, hi = even(2 * base, block), even(2 * base + 1, block)
        g_re = table_a[lo, :] + (table_b[lo, :] + table_c[lo, :])
        g_im = table_a[hi, :] + (table_b[hi, :] + table_c[hi, :])
        new_acc = acc[rows, :] + jnp.sum(g_re * g_re + g_im * g_im, axis=1, keepdims=True) * (1.0 / dim)
        acc_out[rows, :] = new_acc
        scale = LR_ENT * lax.rsqrt(new_acc + ADA_EPS)
        ent_out[lo, :] = ent[lo, :] - g_re * scale
        ent_out[hi, :] = ent[hi, :] - g_im * scale
        return carry

    lax.fori_loop(0, rows_all // 2 // block, step_rows, 0)


def rel_kernel(group, dim, part, rel, racc, rel_out, racc_out, recv, send_sem, recv_sem):
    total = rel_exchange(group, part, recv, send_sem, recv_sem)()
    new_rel, new_acc = rel_update(total, rel[...], racc[...], dim)
    rel_out[...] = new_rel
    racc_out[...] = new_acc


def solution(mesh):
    group = mesh.shape["ent"]
    row_spec = P(("sweep", "ent"))
    table_spec = P(("sweep", "ent"), None)
    edge_spec = P(("sweep", "ent"), None, None)
    rel_spec = P("sweep", None)
    racc_spec = P("sweep")

    def device_step(ent_table, ent_accum, rel_table, rel_accum, head_idx, tail_idx, rel_idx, edge_mask, neg_idx):
        rows, dim = ent_table.shape
        half = dim // 2
        num_rels = rel_table.shape[0]
        rounds, count = head_idx.shape[1:]
        negs = neg_idx.shape[2]
        rels = -(-num_rels // 8) * 8
        keep = -(-(half + 1) // 8) * 8

        def spread(table):
            return jnp.pad(table.reshape(table.shape[0], 2, half), ((0, 0), (0, 0), (0, LANES - half)))

        ent = spread(ent_table).reshape(2 * rows, LANES)
        acc = jnp.broadcast_to(ent_accum[:, None], (rows, LANES))
        rel = jnp.pad(spread(rel_table).reshape(num_rels, 2 * LANES), ((0, rels - num_rels), (0, 0)))
        racc = jnp.broadcast_to(jnp.pad(rel_accum, (0, rels - num_rels))[:, None], (rels, LANES))
        own = jnp.stack([head_idx[0] * 2, rel_idx[0] * 2], axis=1)
        own_rel = jnp.stack([head_idx[0], rel_idx[0]], axis=1)
        away = jnp.stack([tail_idx[0] * 2, neg_idx[0] * 2, edge_mask[0]], axis=1)

        def shape(*dims, dtype=F32):
            return jax.ShapeDtypeStruct(dims, dtype)

        losses = []
        for shift in range(rounds):
            there = [(dev, (dev + shift) % group) for dev in range(group)]
            back = [(dst, src) for src, dst in there]
            incoming = away[shift] if shift == 0 else lax.ppermute(away[shift], "ent", there)
            scratch = [pltpu.VMEM((2 * rels, LANES), F32), pltpu.VMEM((2 * negs, LANES), F32), pltpu.VMEM((2 * count, LANES), F32)]
            q, neg, tail, head, relrow = pl.pallas_call(
                functools.partial(query_kernel, shift),
                out_shape=(shape(count, 2 * LANES, dtype=BF16), shape(negs, 2 * LANES, dtype=BF16), shape(count, 2 * LANES, dtype=BF16),
                           shape(2 * count, LANES), shape(2 * count, LANES)),
                in_specs=[VMEM, VMEM, SMEM, SMEM],
                out_specs=(VMEM,) * 5,
                scratch_shapes=scratch,
                compiler_params=pltpu.CompilerParams(vmem_limit_bytes=24 * MIB),
                name=f"query_{shift}",
            )(ent, rel, own, incoming)
            if shift:
                q = lax.ppermute(q, "ent", there)
            dq, dneg, dtail = pl.pallas_call(
                functools.partial(score_kernel, half),
                out_shape=(shape(2 * keep, count), shape(2 * negs, LANES), shape(2 * count, LANES)),
                in_specs=[VMEM] * 4,
                out_specs=(VMEM,) * 3,
                scratch_shapes=[pltpu.VMEM((2 * LANES, negs), BF16), pltpu.VMEM((negs, 256), F32), pltpu.VMEM((negs, count), BF16)],
                compiler_params=pltpu.CompilerParams(vmem_limit_bytes=32 * MIB),
                name="score",
            )(q, neg, tail, incoming)
            if shift:
                dq = lax.ppermute(dq, "ent", back)
            ent, acc, part, loss = pl.pallas_call(
                functools.partial(update_kernel, dim, shift),
                out_shape=(shape(2 * rows, LANES), shape(rows, LANES), shape(rels, 2 * LANES), shape(8, LANES)),
                in_specs=[VMEM] * 7 + [SMEM, VMEM, SMEM],
                out_specs=(VMEM,) * 4,
                scratch_shapes=[pltpu.VMEM((2 * rows, LANES), F32)] * 3 + [pltpu.VMEM((2 * count, LANES), F32)],
                input_output_aliases={0: 0, 1: 1},
                compiler_params=pltpu.CompilerParams(vmem_limit_bytes=46 * MIB),
                name=f"update_{shift}",
            )(ent, acc, dneg, dtail, dq, head, relrow, own, own_rel, incoming)
            losses.append(loss[0, 0])
            rel, racc = pl.pallas_call(
                functools.partial(rel_kernel, group, dim),
                out_shape=(shape(rels, 2 * LANES), shape(rels, LANES)),
                in_specs=[VMEM] * 3,
                out_specs=(VMEM,) * 2,
                scratch_shapes=[pltpu.VMEM((group, rels, 2 * LANES), F32), pltpu.SemaphoreType.DMA((group,)), pltpu.SemaphoreType.DMA((group,))],
                compiler_params=pltpu.CompilerParams(collective_id=0, has_side_effects=True, vmem_limit_bytes=4 * MIB),
                name="rel_step",
            )(part, rel, racc)
        new_ent = ent.reshape(rows, 2, LANES)[:, :, :half].reshape(rows, dim)
        new_rel = rel[:num_rels].reshape(num_rels, 2, LANES)[:, :, :half].reshape(num_rels, dim)
        return new_ent, acc[:, 0], new_rel, racc[:num_rels, 0], jnp.stack(losses)[None, :]

    return jax.shard_map(device_step, mesh=mesh, in_specs=(table_spec, row_spec, rel_spec, racc_spec, edge_spec, edge_spec, edge_spec, edge_spec, edge_spec), out_specs=(table_spec, row_spec, rel_spec, racc_spec, P(("sweep", "ent"), None)), check_vma=False)
```

time: 1820 us -> 1080 us (0.59)
  other arithmetic: 660 us -> 3.06 us
  Pallas kernels: 0 us -> 603 us
  local copies, waits for them, and re-layouts: 534 us -> 77.1 us
  blocking collectives: 394 us -> 0 us
  waiting for transfers between devices: 60.4 us -> 380 us
  matrix products: 139 us -> 0 us
    pallas_call x0 -> x32, Pallas kernels: none -> 603 us  [the longest x8 212 us: device_step(): pl.pallas_call(functools.partial(update_kernel, dim, shift), out_shape=(s...]
    scatter-add x24 -> x0, other arithmetic: 421 us -> none  [the longest x8 202 us: device_step(): jax.ops.segment_sum(jnp.concatenate([d_tail, d_negrows], axis=0), jnp.con...]
    psum x8 -> x0, blocking collectives: 394 us -> none  [device_step(): lax.psum(jax.ops.segment_sum(d_rel, rels_now, num_segments=num_rels), 'ent')]
    gather x56 -> x0, local copies, waits for them, and re-layouts: 331 us -> none  [the longest x16 104 us: device_step(): head_rows = jnp.take(cur_table, heads_now, axis=0)]
    ppermute x14 -> x21, waiting for transfers between devices: 60.4 us -> 380 us  [the longest x7 225 us: device_step(): dq = lax.ppermute(dq, 'ent', back)]
    dot_general x24 -> x0, matrix products: 139 us -> none  [the longest x8 64 us: bucket_grads(): jnp.dot(d_neg, neg_rows, preferred_element_type=jnp.float32)]
    reduce_sum x32 -> x0, other arithmetic: 59.3 us -> none  [the longest x8 28.4 us: bucket_grads(): log_norm = jax.nn.logsumexp(logits, axis=1)]
    ppermute x14 -> x0, local copies, waits for them, and re-layouts: 58.4 us -> none  [the longest x7 36.3 us: device_step(): lax.ppermute(tail_grad, 'ent', perm=[(sender, (sender + shift) % group_si...]
  transfers between devices with their start and end apart: 14 -> 21, of which waited for: 5 -> 14; matrix products, arithmetic and copies ran while one was open for 21% -> 2% of each run, Pallas kernels for 0% -> 25%
where the time goes in v1:
time: 1080 us
  Pallas kernels  603 us (56%)
  waiting for transfers between devices  380 us (35%)
  local copies, waits for them, and re-layouts  77.1 us (7%)
  starting transfers between devices  15.4 us (1%)
    ppermute x7, waiting for transfers between devices, device_step(): dq = lax.ppermute(dq, 'ent', back)  225 us
    pallas_call x8, Pallas kernels, device_step(): pl.pallas_call(functools.partial(update_kernel, dim, shift), out_shape=(s...  212 us
    pallas_call x8, Pallas kernels, device_step(): pl.pallas_call(functools.partial(score_kernel, half), out_shape=(shape(2...  179 us
    pallas_call x8, Pallas kernels, device_step(): pl.pallas_call(functools.partial(query_kernel, shift), out_shape=(shape(c...  161 us
    ppermute x7, waiting for transfers between devices, device_step(): q = lax.ppermute(q, 'ent', there)  155 us
    pallas_call x8, Pallas kernels, device_step(): pl.pallas_call(functools.partial(rel_kernel, group, dim), out_shape=(shap...  52.1 us
    unnamed x58, local copies, waits for them, and re-layouts  49.6 us
  transfers between devices with their start and end apart: 21, of which 14 were waited for; matrix products, arithmetic and copies ran while one was open for 2% of the time, Pallas kernels for 25%

profile of v1, /device:TPU:112, one launch (start us, length us, event | category | flops | bytes accessed | tf_op | source)
XLA Modules:
  0.0 1080.1 jit_solution(16555470614940752323)
XLA Ops:
  10.7 7.0 copy.39
  21.6 19.0 %query_0.1 = (bf16[2048,256]{1,0:T(8,128)(2,1)S(1)}, bf16[2048,256]{1,0:T(8,128)(2,1)S(1)}, bf16[2048,256]{1,0:T(8,128)(2,1)S(1)}, f32[4096,128]{1,0:T(8,128)S(1)}, f32[4096,128]{1,0:T(8,128)S(1)}) custom-call(f32[8192,128]{1,0:T(8,128)S(1)} %bitcast.41, f32[16,256]{1,0:T(8,128)S(1)} %pad.18.rel, s32[8,2,2048]{2,1,0:T(2,128)S(1)} %pad_add_fusion.1.own_idx, ...), custom_call_target="tpu_custom_call" | custom-call | tf_op jit(solution)/shard_map/query_0/pallas_call | solution.py:309
  42.0 22.3 %score.8 = (f32[208,2048]{1,0:T(8,128)S(1)}, f32[4096,128]{1,0:T(8,128)S(1)}, f32[4096,128]{1,0:T(8,128)S(1)}) custom-call(bf16[2048,256]{1,0:T(8,128)(2,1)S(1)} %get-tuple-element.117.q, bf16[2048,256]{1,0:T(8,128)(2,1)S(1)} %get-tuple-element.118.neg, bf16[2048,256]{1,0:T(8,128)(2,1)S(1)} %get-tuple-element.119.tail, ...), custom_call_target="tpu_custom_call" | custom-call | tf_op jit(solution)/shard_map/score/pallas_call | solution.py:321
  64.9 26.7 %update_0.1 = (f32[8192,128]{1,0:T(8,128)}, f32[4096,128]{1,0:T(8,128)S(1)}, f32[16,256]{1,0:T(8,128)S(1)}, f32[8,128]{1,0:T(8,128)S(1)}) custom-call(f32[8192,128]{1,0:T(8,128)} %bitcast.42, f32[4096,128]{1,0:T(8,128)S(1)} %broadcast_in_dim.6.acc, f32[4096,128]{1,0:T(8,128)S(1)} %get-tuple-element.120.dneg, ...), custom_call_target="tpu_custom_call", output_to_operand_aliasing={{0}: (0, {}), {1}: (1, {})} | custom-call | tf_op jit(solution)/shard_map/update_0/pallas_call | solution.py:332
  91.7 8.6 rel_step.8
  102.5 20.2 %query_1.1 = (bf16[2048,256]{1,0:T(8,128)(2,1)S(1)}, bf16[2048,256]{1,0:T(8,128)(2,1)S(1)}, bf16[2048,256]{1,0:T(8,128)(2,1)S(1)}, f32[4096,128]{1,0:T(8,128)S(1)}, f32[4096,128]{1,0:T(8,128)S(1)}) custom-call(f32[8192,128]{1,0:T(8,128)S(1)} %copy-done.1, f32[16,256]{1,0:T(8,128)S(1)} %get-tuple-element.128.rel, s32[8,2,2048]{2,1,0:T(2,128)S(1)} %pad_add_fusion.1.own_idx, ...), custom_call_target="tpu_custom_call" | custom-call | tf_op jit(solution)/shard_map/query_1/pallas_call | solution.py:309
  125.6 15.3 %collective-permute-done.1.q = bf16[2048,256]{1,0:T(8,128)(2,1)S(1)} collective-permute-done((bf16[2048,256]{1,0:T(8,128)(2,1)S(1)}, bf16[2048,256]{1,0:T(8,128)(2,1)S(1)}, u32[]{:S(2)}, u32[]{:S(2)}) %collective-permute-start.1) | collective-permute-done | bytes 1048608 | tf_op jit(solution)/shard_map/ppermute | solution.py:320
  140.9 22.3 %score.9 = (f32[208,2048]{1,0:T(8,128)S(1)}, f32[4096,128]{1,0:T(8,128)S(1)}, f32[4096,128]{1,0:T(8,128)S(1)}) custom-call(bf16[2048,256]{1,0:T(8,128)(2,1)S(1)} %collective-permute-done.1.q, bf16[2048,256]{1,0:T(8,128)(2,1)S(1)} %get-tuple-element.130.neg, bf16[2048,256]{1,0:T(8,128)(2,1)S(1)} %get-tuple-element.131.tail, ...), custom_call_target="tpu_custom_call" | custom-call | tf_op jit(solution)/shard_map/score/pallas_call | solution.py:321
  163.4 19.2 %collective-permute-done.2.dq = f32[208,2048]{1,0:T(8,128)S(1)} collective-permute-done((f32[208,2048]{1,0:T(8,128)S(1)}, f32[208,2048]{1,0:T(8,128)S(1)}, u32[]{:S(2)}, u32[]{:S(2)}) %collective-permute-start.2) | collective-permute-done | bytes 1703968 | tf_op jit(solution)/shard_map/ppermute | solution.py:331
  182.6 26.4 %update_1.1 = (f32[8192,128]{1,0:T(8,128)}, f32[4096,128]{1,0:T(8,128)S(1)}, f32[16,256]{1,0:T(8,128)S(1)}, f32[8,128]{1,0:T(8,128)S(1)}) custom-call(f32[8192,128]{1,0:T(8,128)} %get-tuple-element.125.ent, f32[4096,128]{1,0:T(8,128)S(1)} %get-tuple-element.126.acc, ...), custom_call_target="tpu_custom_call", output_to_operand_aliasing={{0}: (0, {}), {1}: (1, {})} | custom-call | tf_op jit(solution)/shard_map/update_1/pallas_call | solution.py:332
  209.1 7.1 rel_step.9
  218.4 20.2 %query_2.1 = (bf16[2048,256]{1,0:T(8,128)(2,1)S(1)}, bf16[2048,256]{1,0:T(8,128)(2,1)S(1)}, bf16[2048,256]{1,0:T(8,128)(2,1)S(1)}, f32[4096,128]{1,0:T(8,128)S(1)}, f32[4096,128]{1,0:T(8,128)S(1)}) custom-call(f32[8192,128]{1,0:T(8,128)S(1)} %copy-done.2, f32[16,256]{1,0:T(8,128)S(1)} %get-tuple-element.141.rel, s32[8,2,2048]{2,1,0:T(2,128)S(1)} %pad_add_fusion.1.own_idx, ...), custom_call_target="tpu_custom_call" | custom-call | tf_op jit(solution)/shard_map/query_2/pallas_call | solution.py:309
  241.5 26.2 %collective-permute-done.4.q = bf16[2048,256]{1,0:T(8,128)(2,1)S(1)} collective-permute-done((bf16[2048,256]{1,0:T(8,128)(2,1)S(1)}, bf16[2048,256]{1,0:T(8,128)(2,1)S(1)}, u32[]{:S(2)}, u32[]{:S(2)}) %collective-permute-start.4) | collective-permute-done | bytes 1048608 | tf_op jit(solution)/shard_map/ppermute | solution.py:320
  267.7 22.3 %score.10 = (f32[208,2048]{1,0:T(8,128)S(1)}, f32[4096,128]{1,0:T(8,128)S(1)}, f32[4096,128]{1,0:T(8,128)S(1)}) custom-call(bf16[2048,256]{1,0:T(8,128)(2,1)S(1)} %collective-permute-done.4.q, bf16[2048,256]{1,0:T(8,128)(2,1)S(1)} %get-tuple-element.143.neg, bf16[2048,256]{1,0:T(8,128)(2,1)S(1)} %get-tuple-element.144.tail, ...), custom_call_target="tpu_custom_call" | custom-call | tf_op jit(solution)/shard_map/score/pallas_call | solution.py:321
  290.8 38.0 %collective-permute-done.5.dq = f32[208,2048]{1,0:T(8,128)S(1)} collective-permute-done((f32[208,2048]{1,0:T(8,128)S(1)}, f32[208,2048]{1,0:T(8,128)S(1)}, u32[]{:S(2)}, u32[]{:S(2)}) %collective-permute-start.5) | collective-permute-done | bytes 1703968 | tf_op jit(solution)/shard_map/ppermute | solution.py:331
  328.8 26.4 %update_2.1 = (f32[8192,128]{1,0:T(8,128)}, f32[4096,128]{1,0:T(8,128)S(1)}, f32[16,256]{1,0:T(8,128)S(1)}, f32[8,128]{1,0:T(8,128)S(1)}) custom-call(f32[8192,128]{1,0:T(8,128)} %get-tuple-element.137.ent, f32[4096,128]{1,0:T(8,128)S(1)} %get-tuple-element.138.acc, ...), custom_call_target="tpu_custom_call", output_to_operand_aliasing={{0}: (0, {}), {1}: (1, {})} | custom-call | tf_op jit(solution)/shard_map/update_2/pallas_call | solution.py:332
  355.3 6.1 rel_step.10
  363.5 20.2 %query_3.1 = (bf16[2048,256]{1,0:T(8,128)(2,1)S(1)}, bf16[2048,256]{1,0:T(8,128)(2,1)S(1)}, bf16[2048,256]{1,0:T(8,128)(2,1)S(1)}, f32[4096,128]{1,0:T(8,128)S(1)}, f32[4096,128]{1,0:T(8,128)S(1)}) custom-call(f32[8192,128]{1,0:T(8,128)S(1)} %copy-done.3, f32[16,256]{1,0:T(8,128)S(1)} %get-tuple-element.154.rel, s32[8,2,2048]{2,1,0:T(2,128)S(1)} %pad_add_fusion.1.own_idx, ...), custom_call_target="tpu_custom_call" | custom-call | tf_op jit(solution)/shard_map/query_3/pallas_call | solution.py:309
  386.5 26.9 %collective-permute-done.7.q = bf16[2048,256]{1,0:T(8,128)(2,1)S(1)} collective-permute-done((bf16[2048,256]{1,0:T(8,128)(2,1)S(1)}, bf16[2048,256]{1,0:T(8,128)(2,1)S(1)}, u32[]{:S(2)}, u32[]{:S(2)}) %collective-permute-start.7) | collective-permute-done | bytes 1048608 | tf_op jit(solution)/shard_map/ppermute | solution.py:320
  413.4 22.3 %score.11 = (f32[208,2048]{1,0:T(8,128)S(1)}, f32[4096,128]{1,0:T(8,128)S(1)}, f32[4096,128]{1,0:T(8,128)S(1)}) custom-call(bf16[2048,256]{1,0:T(8,128)(2,1)S(1)} %collective-permute-done.7.q, bf16[2048,256]{1,0:T(8,128)(2,1)S(1)} %get-tuple-element.156.neg, bf16[2048,256]{1,0:T(8,128)(2,1)S(1)} %get-tuple-element.157.tail, ...), custom_call_target="tpu_custom_call" | custom-call | tf_op jit(solution)/shard_map/score/pallas_call | solution.py:321
  439.0 35.9 %collective-permute-done.8.dq = f32[208,2048]{1,0:T(8,128)S(1)} collective-permute-done((f32[208,2048]{1,0:T(8,128)S(1)}, f32[208,2048]{1,0:T(8,128)S(1)}, u32[]{:S(2)}, u32[]{:S(2)}) %collective-permute-start.8) | collective-permute-done | bytes 1703968 | tf_op jit(solution)/shard_map/ppermute | solution.py:331
  475.0 26.4 %update_3.1 = (f32[8192,128]{1,0:T(8,128)}, f32[4096,128]{1,0:T(8,128)S(1)}, f32[16,256]{1,0:T(8,128)S(1)}, f32[8,128]{1,0:T(8,128)S(1)}) custom-call(f32[8192,128]{1,0:T(8,128)} %get-tuple-element.150.ent, f32[4096,128]{1,0:T(8,128)S(1)} %get-tuple-element.151.acc, ...), custom_call_target="tpu_custom_call", output_to_operand_aliasing={{0}: (0, {}), {1}: (1, {})} | custom-call | tf_op jit(solution)/shard_map/update_3/pallas_call | solution.py:332
  501.4 6.1 rel_step.11
  509.7 20.2 %query_4.1 = (bf16[2048,256]{1,0:T(8,128)(2,1)S(1)}, bf16[2048,256]{1,0:T(8,128)(2,1)S(1)}, bf16[2048,256]{1,0:T(8,128)(2,1)S(1)}, f32[4096,128]{1,0:T(8,128)S(1)}, f32[4096,128]{1,0:T(8,128)S(1)}) custom-call(f32[8192,128]{1,0:T(8,128)S(1)} %copy-done.4, f32[16,256]{1,0:T(8,128)S(1)} %get-tuple-element.167.rel, s32[8,2,2048]{2,1,0:T(2,128)S(1)} %pad_add_fusion.1.own_idx, ...), custom_call_target="tpu_custom_call" | custom-call | tf_op jit(solution)/shard_map/query_4/pallas_call | solution.py:309
  533.8 25.7 %collective-permute-done.10.q = bf16[2048,256]{1,0:T(8,128)(2,1)S(1)} collective-permute-done((bf16[2048,256]{1,0:T(8,128)(2,1)S(1)}, bf16[2048,256]{1,0:T(8,128)(2,1)S(1)}, u32[]{:S(2)}, u32[]{:S(2)}) %collective-permute-start.10) | collective-permute-done | bytes 1048608 | tf_op jit(solution)/shard_map/ppermute | solution.py:320
  559.5 22.5 %score.12 = (f32[208,2048]{1,0:T(8,128)S(1)}, f32[4096,128]{1,0:T(8,128)S(1)}, f32[4096,128]{1,0:T(8,128)S(1)}) custom-call(bf16[2048,256]{1,0:T(8,128)(2,1)S(1)} %collective-permute-done.10.q, bf16[2048,256]{1,0:T(8,128)(2,1)S(1)} %get-tuple-element.169.neg, bf16[2048,256]{1,0:T(8,128)(2,1)S(1)} %get-tuple-element.170.tail, ...), custom_call_target="tpu_custom_call" | custom-call | tf_op jit(solution)/shard_map/score/pallas_call | solution.py:321
  584.0 38.0 %collective-permute-done.11.dq = f32[208,2048]{1,0:T(8,128)S(1)} collective-permute-done((f32[208,2048]{1,0:T(8,128)S(1)}, f32[208,2048]{1,0:T(8,128)S(1)}, u32[]{:S(2)}, u32[]{:S(2)}) %collective-permute-start.11) | collective-permute-done | bytes 1703968 | tf_op jit(solution)/shard_map/ppermute | solution.py:331
  622.0 26.4 %update_4.1 = (f32[8192,128]{1,0:T(8,128)}, f32[4096,128]{1,0:T(8,128)S(1)}, f32[16,256]{1,0:T(8,128)S(1)}, f32[8,128]{1,0:T(8,128)S(1)}) custom-call(f32[8192,128]{1,0:T(8,128)} %get-tuple-element.163.ent, f32[4096,128]{1,0:T(8,128)S(1)} %get-tuple-element.164.acc, ...), custom_call_target="tpu_custom_call", output_to_operand_aliasing={{0}: (0, {}), {1}: (1, {})} | custom-call | tf_op jit(solution)/shard_map/update_4/pallas_call | solution.py:332
  648.4 6.1 rel_step.12
  656.7 20.2 %query_5.1 = (bf16[2048,256]{1,0:T(8,128)(2,1)S(1)}, bf16[2048,256]{1,0:T(8,128)(2,1)S(1)}, bf16[2048,256]{1,0:T(8,128)(2,1)S(1)}, f32[4096,128]{1,0:T(8,128)S(1)}, f32[4096,128]{1,0:T(8,128)S(1)}) custom-call(f32[8192,128]{1,0:T(8,128)S(1)} %copy-done.5, f32[16,256]{1,0:T(8,128)S(1)} %get-tuple-element.180.rel, s32[8,2,2048]{2,1,0:T(2,128)S(1)} %pad_add_fusion.1.own_idx, ...), custom_call_target="tpu_custom_call" | custom-call | tf_op jit(solution)/shard_map/query_5/pallas_call | solution.py:309
  680.5 24.5 %collective-permute-done.13.q = bf16[2048,256]{1,0:T(8,128)(2,1)S(1)} collective-permute-done((bf16[2048,256]{1,0:T(8,128)(2,1)S(1)}, bf16[2048,256]{1,0:T(8,128)(2,1)S(1)}, u32[]{:S(2)}, u32[]{:S(2)}) %collective-permute-start.13) | collective-permute-done | bytes 1048608 | tf_op jit(solution)/shard_map/ppermute | solution.py:320
  704.9 22.3 %score.13 = (f32[208,2048]{1,0:T(8,128)S(1)}, f32[4096,128]{1,0:T(8,128)S(1)}, f32[4096,128]{1,0:T(8,128)S(1)}) custom-call(bf16[2048,256]{1,0:T(8,128)(2,1)S(1)} %collective-permute-done.13.q, bf16[2048,256]{1,0:T(8,128)(2,1)S(1)} %get-tuple-element.182.neg, bf16[2048,256]{1,0:T(8,128)(2,1)S(1)} %get-tuple-element.183.tail, ...), custom_call_target="tpu_custom_call" | custom-call | tf_op jit(solution)/shard_map/score/pallas_call | solution.py:321
  729.2 38.4 %collective-permute-done.14.dq = f32[208,2048]{1,0:T(8,128)S(1)} collective-permute-done((f32[208,2048]{1,0:T(8,128)S(1)}, f32[208,2048]{1,0:T(8,128)S(1)}, u32[]{:S(2)}, u32[]{:S(2)}) %collective-permute-start.14) | collective-permute-done | bytes 1703968 | tf_op jit(solution)/shard_map/ppermute | solution.py:331
  767.6 26.4 %update_5.1 = (f32[8192,128]{1,0:T(8,128)}, f32[4096,128]{1,0:T(8,128)S(1)}, f32[16,256]{1,0:T(8,128)S(1)}, f32[8,128]{1,0:T(8,128)S(1)}) custom-call(f32[8192,128]{1,0:T(8,128)} %get-tuple-element.176.ent, f32[4096,128]{1,0:T(8,128)S(1)} %get-tuple-element.177.acc, ...), custom_call_target="tpu_custom_call", output_to_operand_aliasing={{0}: (0, {}), {1}: (1, {})} | custom-call | tf_op jit(solution)/shard_map/update_5/pallas_call | solution.py:332
  794.0 6.1 rel_step.13
  802.3 20.2 %query_6.1 = (bf16[2048,256]{1,0:T(8,128)(2,1)S(1)}, bf16[2048,256]{1,0:T(8,128)(2,1)S(1)}, bf16[2048,256]{1,0:T(8,128)(2,1)S(1)}, f32[4096,128]{1,0:T(8,128)S(1)}, f32[4096,128]{1,0:T(8,128)S(1)}) custom-call(f32[8192,128]{1,0:T(8,128)S(1)} %copy-done.6, f32[16,256]{1,0:T(8,128)S(1)} %get-tuple-element.193.rel, s32[8,2,2048]{2,1,0:T(2,128)S(1)} %pad_add_fusion.1.own_idx, ...), custom_call_target="tpu_custom_call" | custom-call | tf_op jit(solution)/shard_map/query_6/pallas_call | solution.py:309
  826.1 24.4 %collective-permute-done.16.q = bf16[2048,256]{1,0:T(8,128)(2,1)S(1)} collective-permute-done((bf16[2048,256]{1,0:T(8,128)(2,1)S(1)}, bf16[2048,256]{1,0:T(8,128)(2,1)S(1)}, u32[]{:S(2)}, u32[]{:S(2)}) %collective-permute-start.16) | collective-permute-done | bytes 1048608 | tf_op jit(solution)/shard_map/ppermute | solution.py:320
  850.4 22.3 %score.14 = (f32[208,2048]{1,0:T(8,128)S(1)}, f32[4096,128]{1,0:T(8,128)S(1)}, f32[4096,128]{1,0:T(8,128)S(1)}) custom-call(bf16[2048,256]{1,0:T(8,128)(2,1)S(1)} %collective-permute-done.16.q, bf16[2048,256]{1,0:T(8,128)(2,1)S(1)} %get-tuple-element.195.neg, bf16[2048,256]{1,0:T(8,128)(2,1)S(1)} %get-tuple-element.196.tail, ...), custom_call_target="tpu_custom_call" | custom-call | tf_op jit(solution)/shard_map/score/pallas_call | solution.py:321
  874.6 37.8 %collective-permute-done.17.dq = f32[208,2048]{1,0:T(8,128)S(1)} collective-permute-done((f32[208,2048]{1,0:T(8,128)S(1)}, f32[208,2048]{1,0:T(8,128)S(1)}, u32[]{:S(2)}, u32[]{:S(2)}) %collective-permute-start.17) | collective-permute-done | bytes 1703968 | tf_op jit(solution)/shard_map/ppermute | solution.py:331
  912.4 26.4 %update_6.1 = (f32[8192,128]{1,0:T(8,128)}, f32[4096,128]{1,0:T(8,128)S(1)}, f32[16,256]{1,0:T(8,128)S(1)}, f32[8,128]{1,0:T(8,128)S(1)}) custom-call(f32[8192,128]{1,0:T(8,128)} %get-tuple-element.189.ent, f32[4096,128]{1,0:T(8,128)S(1)} %get-tuple-element.190.acc, ...), custom_call_target="tpu_custom_call", output_to_operand_aliasing={{0}: (0, {}), {1}: (1, {})} | custom-call | tf_op jit(solution)/shard_map/update_6/pallas_call | solution.py:332
  938.8 6.1 rel_step.14
  947.1 20.2 %query_7.1 = (bf16[2048,256]{1,0:T(8,128)(2,1)S(1)}, bf16[2048,256]{1,0:T(8,128)(2,1)S(1)}, bf16[2048,256]{1,0:T(8,128)(2,1)S(1)}, f32[4096,128]{1,0:T(8,128)S(1)}, f32[4096,128]{1,0:T(8,128)S(1)}) custom-call(f32[8192,128]{1,0:T(8,128)S(1)} %copy-done.7, f32[16,256]{1,0:T(8,128)S(1)} %get-tuple-element.206.rel, s32[8,2,2048]{2,1,0:T(2,128)S(1)} %pad_add_fusion.1.own_idx, ...), custom_call_target="tpu_custom_call" | custom-call | tf_op jit(solution)/shard_map/query_7/pallas_call | solution.py:309
  970.6 12.3 %collective-permute-done.19.q = bf16[2048,256]{1,0:T(8,128)(2,1)S(1)} collective-permute-done((bf16[2048,256]{1,0:T(8,128)(2,1)S(1)}, bf16[2048,256]{1,0:T(8,128)(2,1)S(1)}, u32[]{:S(2)}, u32[]{:S(2)}) %collective-permute-start.19) | collective-permute-done | bytes 1048608 | tf_op jit(solution)/shard_map/ppermute | solution.py:320
  982.9 22.3 %score.15 = (f32[208,2048]{1,0:T(8,128)S(1)}, f32[4096,128]{1,0:T(8,128)S(1)}, f32[4096,128]{1,0:T(8,128)S(1)}) custom-call(bf16[2048,256]{1,0:T(8,128)(2,1)S(1)} %collective-permute-done.19.q, bf16[2048,256]{1,0:T(8,128)(2,1)S(1)} %get-tuple-element.208.neg, bf16[2048,256]{1,0:T(8,128)(2,1)S(1)} %get-tuple-element.209.tail, ...), custom_call_target="tpu_custom_call" | custom-call | tf_op jit(solution)/shard_map/score/pallas_call | solution.py:321
  1010.5 17.4 %collective-permute-done.20.dq = f32[208,2048]{1,0:T(8,128)S(1)} collective-permute-done((f32[208,2048]{1,0:T(8,128)S(1)}, f32[208,2048]{1,0:T(8,128)S(1)}, u32[]{:S(2)}, u32[]{:S(2)}) %collective-permute-start.20) | collective-permute-done | bytes 1703968 | tf_op jit(solution)/shard_map/ppermute | solution.py:331
  1027.9 26.4 %update_7.1 = (f32[8192,128]{1,0:T(8,128)}, f32[4096,128]{1,0:T(8,128)S(1)}, f32[16,256]{1,0:T(8,128)S(1)}, f32[8,128]{1,0:T(8,128)S(1)}) custom-call(f32[8192,128]{1,0:T(8,128)} %get-tuple-element.202.ent, f32[4096,128]{1,0:T(8,128)S(1)} %get-tuple-element.203.acc, ...), custom_call_target="tpu_custom_call", output_to_operand_aliasing={{0}: (0, {}), {1}: (1, {})} | custom-call | tf_op jit(solution)/shard_map/update_7/pallas_call | solution.py:332
  1054.8 6.1 rel_step.15
  1062.2 7.2 copy.38
  (117 shorter events, 81.3 us)
Async XLA Ops:
  3.6 96.8 %collective-permute-start = (s32[3,2048]{1,0:T(4,128)S(1)}, s32[3,2048]{1,0:T(4,128)S(1)}, u32[]{:S(2)}, u32[]{:S(2)}) collective-permute-start(s32[3,2048]{1,0:T(4,128)S(1)} %get-tuple-element.235), channel_id=1, source_target_pairs={{0,1},{1,2},{2,3},{3,4},{4,5},{5,6},{6,7},{7,0},{8,9},{9,10},{10,1... | collective-permute-start | bytes 73736 | tf_op jit(solution)/shard_map/ppermute | solution.py:307
  10.7 7.0 copy-start.25
  17.8 3.7 copy-start.26
  21.5 19.1 %copy-start = (f32[4096,2,128]{2,1,0:T(2,128)}, f32[4096,2,128]{2,1,0:T(2,128)S(1)}, u32[]{:S(2)}) copy-start(f32[4096,2,128]{2,1,0:T(2,128)S(1)} %pad.16.clone) | copy-start | bytes 12582916
  40.6 1.4 copy-start.23
  42.0 22.9 %copy-start.22 = (f32[4096,128]{1,0:T(8,128)}, f32[4096,128]{1,0:T(8,128)S(1)}, u32[]{:S(2)}) copy-start(f32[4096,128]{1,0:T(8,128)S(1)} %get-tuple-element.123.head) | copy-start | bytes 6291460
  42.0 22.3 %copy-start.24 = (f32[4096]{0:T(1024)S(1)}, f32[4096]{0:T(1024)}, u32[]{:S(2)}) copy-start(f32[4096]{0:T(1024)} %param.10) | copy-start | bytes 49156
  100.4 2.2 copy-start.1
  122.8 1.3 copy-start.12
  124.1 1.4 copy-start.13
  125.5 15.4 %collective-permute-start.1 = (bf16[2048,256]{1,0:T(8,128)(2,1)S(1)}, bf16[2048,256]{1,0:T(8,128)(2,1)S(1)}, u32[]{:S(2)}, u32[]{:S(2)}) collective-permute-start(bf16[2048,256]{1,0:T(8,128)(2,1)S(1)} %get-tuple-element.129), channel_id=1, source_target_pairs={{0,1},{1,2},{2,3},{3,4},{4,5},{5,6},{6,7},{7,0},{8,9},{9,10},{10,1... | collective-permute-start | bytes 3145736 | tf_op jit(solution)/shard_map/ppermute | solution.py:320
  163.2 19.4 %collective-permute-start.2 = (f32[208,2048]{1,0:T(8,128)S(1)}, f32[208,2048]{1,0:T(8,128)S(1)}, u32[]{:S(2)}, u32[]{:S(2)}) collective-permute-start(f32[208,2048]{1,0:T(8,128)S(1)} %get-tuple-element.134), channel_id=1, source_target_pairs={{1,0},{2,1},{3,2},{4,3},{5,4},{6,5},{7,6},{0,7},{9,8},{10,9},{11,1... | collective-permute-start | bytes 5111816 | tf_op jit(solution)/shard_map/ppermute | solution.py:331
  163.3 52.9 %collective-permute-start.3 = (s32[3,2048]{1,0:T(4,128)S(1)}, s32[3,2048]{1,0:T(4,128)S(1)}, u32[]{:S(2)}, u32[]{:S(2)}) collective-permute-start(s32[3,2048]{1,0:T(4,128)S(1)} %get-tuple-element.234), channel_id=1, source_target_pairs={{0,2},{1,3},{2,4},{3,5},{4,6},{5,7},{6,0},{7,1},{8,10},{9,11},{10,... | collective-permute-start | bytes 73736 | tf_op jit(solution)/shard_map/ppermute | solution.py:307
  216.2 2.2 copy-start.2
  238.7 1.3 copy-start.14
  240.0 1.4 copy-start.15
  241.3 26.4 %collective-permute-start.4 = (bf16[2048,256]{1,0:T(8,128)(2,1)S(1)}, bf16[2048,256]{1,0:T(8,128)(2,1)S(1)}, u32[]{:S(2)}, u32[]{:S(2)}) collective-permute-start(bf16[2048,256]{1,0:T(8,128)(2,1)S(1)} %get-tuple-element.142), channel_id=1, source_target_pairs={{0,2},{1,3},{2,4},{3,5},{4,6},{5,7},{6,0},{7,1},{8,10},{9,11},{10,... | collective-permute-start | bytes 3145736 | tf_op jit(solution)/shard_map/ppermute | solution.py:320
  290.1 38.8 %collective-permute-start.5 = (f32[208,2048]{1,0:T(8,128)S(1)}, f32[208,2048]{1,0:T(8,128)S(1)}, u32[]{:S(2)}, u32[]{:S(2)}) collective-permute-start(f32[208,2048]{1,0:T(8,128)S(1)} %get-tuple-element.147), channel_id=1, source_target_pairs={{2,0},{3,1},{4,2},{5,3},{6,4},{7,5},{0,6},{1,7},{10,8},{11,9},{12,... | collective-permute-start | bytes 5111816 | tf_op jit(solution)/shard_map/ppermute | solution.py:331
  290.8 70.5 %collective-permute-start.6 = (s32[3,2048]{1,0:T(4,128)S(1)}, s32[3,2048]{1,0:T(4,128)S(1)}, u32[]{:S(2)}, u32[]{:S(2)}) collective-permute-start(s32[3,2048]{1,0:T(4,128)S(1)} %get-tuple-element.233), channel_id=1, source_target_pairs={{0,3},{1,4},{2,5},{3,6},{4,7},{5,0},{6,1},{7,2},{8,11},{9,12},{10,... | collective-permute-start | bytes 73736 | tf_op jit(solution)/shard_map/ppermute | solution.py:307
  361.4 2.2 copy-start.3
  383.8 1.3 copy-start.16
  385.1 1.4 copy-start.17
  386.5 26.9 %collective-permute-start.7 = (bf16[2048,256]{1,0:T(8,128)(2,1)S(1)}, bf16[2048,256]{1,0:T(8,128)(2,1)S(1)}, u32[]{:S(2)}, u32[]{:S(2)}) collective-permute-start(bf16[2048,256]{1,0:T(8,128)(2,1)S(1)} %get-tuple-element.155), channel_id=1, source_target_pairs={{0,3},{1,4},{2,5},{3,6},{4,7},{5,0},{6,1},{7,2},{8,11},{9,12},{10,... | collective-permute-start | bytes 3145736 | tf_op jit(solution)/shard_map/ppermute | solution.py:320
  435.7 39.3 %collective-permute-start.8 = (f32[208,2048]{1,0:T(8,128)S(1)}, f32[208,2048]{1,0:T(8,128)S(1)}, u32[]{:S(2)}, u32[]{:S(2)}) collective-permute-start(f32[208,2048]{1,0:T(8,128)S(1)} %get-tuple-element.160), channel_id=1, source_target_pairs={{3,0},{4,1},{5,2},{6,3},{7,4},{0,5},{1,6},{2,7},{11,8},{12,9},{13,... | collective-permute-start | bytes 5111816 | tf_op jit(solution)/shard_map/ppermute | solution.py:331
  436.1 71.3 %collective-permute-start.9 = (s32[3,2048]{1,0:T(4,128)S(1)}, s32[3,2048]{1,0:T(4,128)S(1)}, u32[]{:S(2)}, u32[]{:S(2)}) collective-permute-start(s32[3,2048]{1,0:T(4,128)S(1)} %get-tuple-element.232), channel_id=1, source_target_pairs={{0,4},{1,5},{2,6},{3,7},{4,0},{5,1},{6,2},{7,3},{8,12},{9,13},{10,... | collective-permute-start | bytes 73736 | tf_op jit(solution)/shard_map/ppermute | solution.py:307
  507.5 2.2 copy-start.4
  529.9 1.3 copy-start.18
  531.2 1.4 copy-start.19
  532.6 26.9 %collective-permute-start.10 = (bf16[2048,256]{1,0:T(8,128)(2,1)S(1)}, bf16[2048,256]{1,0:T(8,128)(2,1)S(1)}, u32[]{:S(2)}, u32[]{:S(2)}) collective-permute-start(bf16[2048,256]{1,0:T(8,128)(2,1)S(1)} %get-tuple-element.168), channel_id=1, source_target_pairs={{0,4},{1,5},{2,6},{3,7},{4,0},{5,1},{6,2},{7,3},{8,12},{9,13},{10,... | collective-permute-start | bytes 3145736 | tf_op jit(solution)/shard_map/ppermute | solution.py:320
  582.0 39.9 %collective-permute-start.11 = (f32[208,2048]{1,0:T(8,128)S(1)}, f32[208,2048]{1,0:T(8,128)S(1)}, u32[]{:S(2)}, u32[]{:S(2)}) collective-permute-start(f32[208,2048]{1,0:T(8,128)S(1)} %get-tuple-element.173), channel_id=1, source_target_pairs={{4,0},{5,1},{6,2},{7,3},{0,4},{1,5},{2,6},{3,7},{12,8},{13,9},{14,... | collective-permute-start | bytes 5111816 | tf_op jit(solution)/shard_map/ppermute | solution.py:331
  583.3 71.2 %collective-permute-start.12 = (s32[3,2048]{1,0:T(4,128)S(1)}, s32[3,2048]{1,0:T(4,128)S(1)}, u32[]{:S(2)}, u32[]{:S(2)}) collective-permute-start(s32[3,2048]{1,0:T(4,128)S(1)} %get-tuple-element.231), channel_id=1, source_target_pairs={{0,5},{1,6},{2,7},{3,0},{4,1},{5,2},{6,3},{7,4},{8,13},{9,14},{10,... | collective-permute-start | bytes 73736 | tf_op jit(solution)/shard_map/ppermute | solution.py:307
  654.5 2.2 copy-start.5
  676.9 1.3 copy-start.20
  678.2 1.4 copy-start.21
  679.6 25.3 %collective-permute-start.13 = (bf16[2048,256]{1,0:T(8,128)(2,1)S(1)}, bf16[2048,256]{1,0:T(8,128)(2,1)S(1)}, u32[]{:S(2)}, u32[]{:S(2)}) collective-permute-start(bf16[2048,256]{1,0:T(8,128)(2,1)S(1)} %get-tuple-element.181), channel_id=1, source_target_pairs={{0,5},{1,6},{2,7},{3,0},{4,1},{5,2},{6,3},{7,4},{8,13},{9,14},{10,... | collective-permute-start | bytes 3145736 | tf_op jit(solution)/shard_map/ppermute | solution.py:320
  727.2 40.4 %collective-permute-start.14 = (f32[208,2048]{1,0:T(8,128)S(1)}, f32[208,2048]{1,0:T(8,128)S(1)}, u32[]{:S(2)}, u32[]{:S(2)}) collective-permute-start(f32[208,2048]{1,0:T(8,128)S(1)} %get-tuple-element.186), channel_id=1, source_target_pairs={{5,0},{6,1},{7,2},{0,3},{1,4},{2,5},{3,6},{4,7},{13,8},{14,9},{15,... | collective-permute-start | bytes 5111816 | tf_op jit(solution)/shard_map/ppermute | solution.py:331
  727.4 72.7 %collective-permute-start.15 = (s32[3,2048]{1,0:T(4,128)S(1)}, s32[3,2048]{1,0:T(4,128)S(1)}, u32[]{:S(2)}, u32[]{:S(2)}) collective-permute-start(s32[3,2048]{1,0:T(4,128)S(1)} %get-tuple-element.230), channel_id=1, source_target_pairs={{0,6},{1,7},{2,0},{3,1},{4,2},{5,3},{6,4},{7,5},{8,14},{9,15},{10,... | collective-permute-start | bytes 73736 | tf_op jit(solution)/shard_map/ppermute | solution.py:307
  800.1 2.2 copy-start.6
  822.6 1.3 copy-start.10
  823.9 1.4 copy-start.11
  825.2 25.2 %collective-permute-start.16 = (bf16[2048,256]{1,0:T(8,128)(2,1)S(1)}, bf16[2048,256]{1,0:T(8,128)(2,1)S(1)}, u32[]{:S(2)}, u32[]{:S(2)}) collective-permute-start(bf16[2048,256]{1,0:T(8,128)(2,1)S(1)} %get-tuple-element.194), channel_id=1, source_target_pairs={{0,6},{1,7},{2,0},{3,1},{4,2},{5,3},{6,4},{7,5},{8,14},{9,15},{10,... | collective-permute-start | bytes 3145736 | tf_op jit(solution)/shard_map/ppermute | solution.py:320
  872.7 39.7 %collective-permute-start.17 = (f32[208,2048]{1,0:T(8,128)S(1)}, f32[208,2048]{1,0:T(8,128)S(1)}, u32[]{:S(2)}, u32[]{:S(2)}) collective-permute-start(f32[208,2048]{1,0:T(8,128)S(1)} %get-tuple-element.199), channel_id=1, source_target_pairs={{6,0},{7,1},{0,2},{1,3},{2,4},{3,5},{4,6},{5,7},{14,8},{15,9},{8,1... | collective-permute-start | bytes 5111816 | tf_op jit(solution)/shard_map/ppermute | solution.py:331
  873.0 71.9 %collective-permute-start.18 = (s32[3,2048]{1,0:T(4,128)S(1)}, s32[3,2048]{1,0:T(4,128)S(1)}, u32[]{:S(2)}, u32[]{:S(2)}) collective-permute-start(s32[3,2048]{1,0:T(4,128)S(1)} %get-tuple-element.229), channel_id=1, source_target_pairs={{0,7},{1,0},{2,1},{3,2},{4,3},{5,4},{6,5},{7,6},{8,15},{9,8},{10,9... | collective-permute-start | bytes 73736 | tf_op jit(solution)/shard_map/ppermute | solution.py:307
  944.9 2.2 copy-start.7
  967.4 1.3 copy-start.8
  968.7 1.4 copy-start.9
  970.0 12.8 %collective-permute-start.19 = (bf16[2048,256]{1,0:T(8,128)(2,1)S(1)}, bf16[2048,256]{1,0:T(8,128)(2,1)S(1)}, u32[]{:S(2)}, u32[]{:S(2)}) collective-permute-start(bf16[2048,256]{1,0:T(8,128)(2,1)S(1)} %get-tuple-element.207), channel_id=1, source_target_pairs={{0,7},{1,0},{2,1},{3,2},{4,3},{5,4},{6,5},{7,6},{8,15},{9,8},{10,9... | collective-permute-start | bytes 3145736 | tf_op jit(solution)/shard_map/ppermute | solution.py:320
  1005.2 22.7 %collective-permute-start.20 = (f32[208,2048]{1,0:T(8,128)S(1)}, f32[208,2048]{1,0:T(8,128)S(1)}, u32[]{:S(2)}, u32[]{:S(2)}) collective-permute-start(f32[208,2048]{1,0:T(8,128)S(1)} %get-tuple-element.212), channel_id=1, source_target_pairs={{7,0},{0,1},{1,2},{2,3},{3,4},{4,5},{5,6},{6,7},{15,8},{8,9},{9,10... | collective-permute-start | bytes 5111816 | tf_op jit(solution)/shard_map/ppermute | solution.py:331
